TPU v7x, 32 devices: a whole 2x2x4 slice. The times are simulated.
32 devices in a mesh: dp: 4 (over z), blk: 4 (over y, core), aa: 2 (over x).
Axes of the slice: x: 2, y: 2, z: 4, core: 2. Of those that a mesh axis runs over, the one named last changes fastest.
Arguments:
- queries: bfloat16 [4, 1024, 2048], P('dp', ('blk', 'aa')), may hold values from -128 to 128
- keys: bfloat16 [4, 1024, 512], P('dp', ('blk', 'aa')), may hold values from -10 to 10
- values: bfloat16 [4, 1024, 512], P('dp', ('blk', 'aa')), may hold values from -6 to 6
- grad_parts: float32 [4, 8, 131072], P('dp', ('blk', 'aa')), may hold values from -192 to 192
Outputs:
- attended: bfloat16 [4, 1024, 2048], P('dp', 'blk', 'aa')
- grad_mean: float32 [131072], P(('blk', 'aa'))
All inputs are finite; a program needn't handle non-finite values.
Results may differ from a plain program's by a relative error of at most 0.008.
Values may be sent and summed in bfloat16 or wider, within the bound.
A program may use at most 64 MiB of HBM per device.

v0:
```python
import jax
import jax.numpy as jnp
from jax import lax
from jax.sharding import PartitionSpec as P

HQ = 16
KVH = 4
DH = 128


def shifted(value, axis, by):
    peers = lax.axis_size(axis)
    pairs = [(i, i + by) for i in range(peers) if 0 <= i + by < peers]
    return lax.ppermute(value, axis, pairs)


def attend(queries, keys, values):
    rows = queries.shape[0]
    size_aa = lax.axis_size("aa")
    spread = max(KVH, size_aa)
    q_heads = queries.reshape(rows, HQ, DH)
    k_heads = jnp.repeat(keys.reshape(rows, KVH, DH), spread // KVH, axis=1)
    v_heads = jnp.repeat(values.reshape(rows, KVH, DH), spread // KVH, axis=1)
    q_here, k_here, v_here = (
        lax.all_to_all(q_heads, "aa", split_axis=1, concat_axis=0, tiled=True),
        lax.all_to_all(k_heads, "aa", split_axis=1, concat_axis=0, tiled=True),
        lax.all_to_all(v_heads, "aa", split_axis=1, concat_axis=0, tiled=True),
    )
    span = q_here.shape[0]
    reach = span // 4
    prior_k, prior_v = shifted((k_here[span - reach :], v_here[span - reach :]), "blk", 1)
    group = q_here.shape[1] // k_here.shape[1]
    k_all = jnp.repeat(jnp.concatenate([prior_k, k_here], 0), group, axis=1)
    v_all = jnp.repeat(jnp.concatenate([prior_v, v_here], 0), group, axis=1)
    step_rows = min(256, reach)
    anchor = lax.axis_index("blk") * span
    scale = DH ** (-0.5)

    def one_block(index):
        offset = index * step_rows
        q_block = lax.dynamic_slice_in_dim(q_here, offset, step_rows, 0)
        k_block = lax.dynamic_slice_in_dim(k_all, offset, step_rows + reach, 0)
        v_block = lax.dynamic_slice_in_dim(v_all, offset, step_rows + reach, 0)
        scores = (
            jnp.einsum("qhd,khd->hqk", q_block, k_block, preferred_element_type=jnp.float32) * scale
        )
        q_pos = anchor + offset + jnp.arange(step_rows, dtype=jnp.int32)
        k_pos = anchor + offset - reach + jnp.arange(step_rows + reach, dtype=jnp.int32)
        allowed = (k_pos[None, :] <= q_pos[:, None]) & (k_pos[None, :] > q_pos[:, None] - reach)
        scores = jnp.where(allowed[None], scores, -1e30)
        top = jnp.max(scores, axis=-1, keepdims=True)
        expo = jnp.exp(scores - top)
        weights = (expo / jnp.sum(expo, axis=-1, keepdims=True)).astype(jnp.bfloat16)
        out = jnp.einsum("hqk,khd->qhd", weights, v_block, preferred_element_type=jnp.float32)
        return out.astype(jnp.bfloat16)

    blocks = lax.map(one_block, jnp.arange(span // step_rows, dtype=jnp.int32))
    return blocks.reshape(span, -1)


def average(grad_parts):
    members = lax.axis_size("blk") * lax.axis_size("aa")
    replicas = lax.axis_size("dp")
    flat_grad = grad_parts.reshape(-1)
    share = lax.psum_scatter(flat_grad, ("blk", "aa"), scatter_dimension=0, tiled=True)
    total = lax.psum(share, "dp")
    return total / (members * replicas)


def shards(queries, keys, values, grad_parts):
    attended = attend(queries[0], keys[0], values[0])[None]
    grad_mean = average(grad_parts)
    return (attended, grad_mean)


def solution(mesh):
    placed = (
        P("dp", ("blk", "aa"), None),
        P("dp", ("blk", "aa"), None),
        P("dp", ("blk", "aa"), None),
        P("dp", ("blk", "aa"), None),
    )
    return jax.shard_map(
        shards,
        mesh=mesh,
        in_specs=placed,
        out_specs=(P("dp", "blk", "aa"), P(("blk", "aa"))),
        check_vma=False,
    )
```

profile of v0, /device:TPU:0, one launch (start us, length us, event | category | flops | bytes accessed | tf_op | source)
XLA Modules:
  0.0 135.1 jit_solution(9205147777204657953)
XLA Ops:
  7.2 1.0 copy.38
  8.2 0.8 copy.39
  9.0 4.4 %all-to-all-start.2 = ((bf16[128,4,128]{2,0,1:T(8,128)(2,1)}), bf16[128,4,128]{2,0,1:T(8,128)(2,1)S(1)}, u32[]{:S(2)}, u32[]{:S(2)}) async-start(bf16[128,4,128]{2,0,1:T(8,128)(2,1)} %copy.39), calls=%async_computation.2 | async-start | bytes 262144 | tf_op jit(solution)/shard_map/all_to_all | solution.py:26
  13.5 0.8 copy.32
  14.2 3.7 %all-to-all-done.2 = bf16[128,4,128]{2,0,1:T(8,128)(2,1)S(1)} async-done(((bf16[128,4,128]{2,0,1:T(8,128)(2,1)}), bf16[128,4,128]{2,0,1:T(8,128)(2,1)S(1)}, u32[]{:S(2)}, u32[]{:S(2)}) %all-to-all-start.2) | async-done | bytes 131104 | tf_op jit(solution)/shard_map/all_to_all | solution.py:26
  17.9 3.4 %all-to-all-start = ((bf16[128,4,128]{2,0,1:T(8,128)(2,1)}), bf16[128,4,128]{2,0,1:T(8,128)(2,1)S(1)}, u32[]{:S(2)}, u32[]{:S(2)}) async-start(bf16[128,4,128]{2,0,1:T(8,128)(2,1)} %copy.32), calls=%async_computation | async-start | bytes 262144 | tf_op jit(solution)/shard_map/all_to_all | solution.py:27
  21.3 1.3 collective-permute-start.1
  22.6 0.3 copy.34
  22.9 1.0 copy.35
  23.9 1.8 %all-to-all-done = bf16[128,4,128]{2,0,1:T(8,128)(2,1)S(1)} async-done(((bf16[128,4,128]{2,0,1:T(8,128)(2,1)}), bf16[128,4,128]{2,0,1:T(8,128)(2,1)S(1)}, u32[]{:S(2)}, u32[]{:S(2)}) %all-to-all-start) | async-done | bytes 131104 | tf_op jit(solution)/shard_map/all_to_all | solution.py:27
  25.7 3.5 %all-to-all-start.1 = ((bf16[128,16,128]{2,0,1:T(8,128)(2,1)}), bf16[128,16,128]{2,0,1:T(8,128)(2,1)S(1)}, u32[]{:S(2)}, u32[]{:S(2)}) async-start(bf16[128,16,128]{2,0,1:T(8,128)(2,1)} %copy.35), calls=%async_computation.1 | async-start | bytes 1048576 | tf_op jit(solution)/shard_map/all_to_all | solution.py:25
  29.3 0.7 all-reduce.6.cloned.1.call-update
  30.0 0.6 copy-done.2
  30.7 0.6 dynamic-slice
  32.0 2.9 %collective-permute-start = (bf16[64,2,128]{2,0,1:T(8,128)(2,1)S(1)}, bf16[64,2,128]{2,0,1:T(8,128)(2,1)S(1)}, u32[]{:S(2)}, u32[]{:S(2)}) collective-permute-start(bf16[64,2,128]{2,0,1:T(8,128)(2,1)S(1)} %slice.8), channel_id=1, source_target_pairs={{0,2},{2,4},{4,6},{1,3},{3,5},{5,7},{8,10},{10,12},{12,14},{9,11},... | collective-permute-start | bytes 98312 | tf_op jit(solution)/shard_map/ppermute | solution.py:14
  34.9 0.8 collective-permute-done
  35.7 2.7 %all-to-all-done.1 = bf16[128,16,128]{2,0,1:T(8,128)(2,1)S(1)} async-done(((bf16[128,16,128]{2,0,1:T(8,128)(2,1)}), bf16[128,16,128]{2,0,1:T(8,128)(2,1)S(1)}, u32[]{:S(2)}, u32[]{:S(2)}) %all-to-all-start.1) | async-done | bytes 524320 | tf_op jit(solution)/shard_map/all_to_all | solution.py:25
  38.4 0.3 copy.37
  38.7 51.6 %all-reduce.6.cloned.1.call-done = f32[131072]{0:T(1024)} async-done(((f32[131072]{0:T(1024)}), f32[131072]{0:T(1024)}) %all-reduce.6.cloned.1.call-update) | async-done | bytes 524304
  90.3 1.5 %dynamic-slice.1 = f32[16384]{0:T(1024)} dynamic-slice(f32[131072]{0:T(1024)} %all-reduce.6.cloned.1.call-done, u32[]{:T(128)S(6)} %multiply.2), dynamic_slice_sizes={16384} | dynamic-slice | bytes 131076
  91.9 9.1 %while.13 = (s32[]{:T(128)}, bf16[4,64,8,128]{3,2,1,0:T(8,128)(2,1)S(1)}, s32[4]{0:T(128)S(1)}, bf16[320,8,128]{2,0,1:T(8,128)(2,1)S(1)}, s32[]{:T(128)}, /*inde...) while((s32[]{:T(128)}, ...), condition=%wide.region_3.4_spmd, body=%wide.region_0.3_spmd.sunk | while | flops 34038152 | bytes 1859840 | solution.py:57
  92.0 0.6 dynamic_slice.47
  93.4 0.5 fusion.37
  94.2 0.6 dynamic_slice.47
  95.6 0.5 fusion.37
  96.5 0.6 dynamic_slice.47
  97.9 0.5 fusion.37
  98.8 0.6 dynamic_slice.47
  100.2 0.5 fusion.37
  101.0 1.0 broadcast_in_dim_reshape.3
  102.0 24.8 %all-reduce.4.cloned.1.call-done = f32[16384]{0:T(1024)} async-done(((f32[16384]{0:T(1024)}), f32[16384]{0:T(1024)}) %all-reduce.4.cloned.1.call-update) | async-done | bytes 65552 | tf_op jit(solution)/shard_map/psum | solution.py:66
  126.8 1.5 %broadcast_multiply_fusion = f32[16384]{0:T(1024)} fusion(f32[16384]{0:T(1024)} %all-reduce.4.cloned.1.call-done), kind=kLoop, calls=%fused_computation.26 | loop fusion | flops 16384 | bytes 131072 | tf_op jit(solution)/shard_map/div | solution.py:67
  (44 shorter events, 2.4 us)
Async XLA Ops:
  9.0 4.4 %copy-start.1 = (bf16[1,128,512]{2,1,0:T(8,128)(2,1)S(1)}, bf16[1,128,512]{2,1,0:T(8,128)(2,1)}, u32[]{:S(2)}) copy-start(bf16[1,128,512]{2,1,0:T(8,128)(2,1)} %param.8) | copy-start | bytes 393220
  9.0 8.9 %all-to-all-start.2 = ((bf16[128,4,128]{2,0,1:T(8,128)(2,1)}), bf16[128,4,128]{2,0,1:T(8,128)(2,1)S(1)}, u32[]{:S(2)}, u32[]{:S(2)}) async-start(bf16[128,4,128]{2,0,1:T(8,128)(2,1)} %copy.39), calls=%async_computation.2 | async-start | bytes 262144 | tf_op jit(solution)/shard_map/all_to_all | solution.py:26
  13.3 9.3 %copy-start = (bf16[1,128,2048]{2,1,0:T(8,128)(2,1)S(1)}, bf16[1,128,2048]{2,1,0:T(8,128)(2,1)}, u32[]{:S(2)}) copy-start(bf16[1,128,2048]{2,1,0:T(8,128)(2,1)} %param.6) | copy-start | bytes 1572868
  17.9 7.8 %all-to-all-start = ((bf16[128,4,128]{2,0,1:T(8,128)(2,1)}), bf16[128,4,128]{2,0,1:T(8,128)(2,1)S(1)}, u32[]{:S(2)}, u32[]{:S(2)}) async-start(bf16[128,4,128]{2,0,1:T(8,128)(2,1)} %copy.32), calls=%async_computation | async-start | bytes 262144 | tf_op jit(solution)/shard_map/all_to_all | solution.py:27
  21.3 13.5 %collective-permute-start.1 = (bf16[64,2,128]{2,0,1:T(8,128)(2,1)S(1)}, bf16[64,2,128]{2,0,1:T(8,128)(2,1)S(1)}, u32[]{:S(2)}, u32[]{:S(2)}) collective-permute-start(bf16[64,2,128]{2,0,1:T(8,128)(2,1)S(1)} %slice.9), channel_id=1, source_target_pairs={{0,2},{2,4},{4,6},{1,3},{3,5},{5,7},{8,10},{10,12},{12,14},{9,11},... | collective-permute-start | bytes 98312 | tf_op jit(solution)/shard_map/ppermute | solution.py:14
  25.7 12.6 %all-to-all-start.1 = ((bf16[128,16,128]{2,0,1:T(8,128)(2,1)}), bf16[128,16,128]{2,0,1:T(8,128)(2,1)S(1)}, u32[]{:S(2)}, u32[]{:S(2)}) async-start(bf16[128,16,128]{2,0,1:T(8,128)(2,1)} %copy.35), calls=%async_computation.1 | async-start | bytes 1048576 | tf_op jit(solution)/shard_map/all_to_all | solution.py:25
  29.2 61.0 %all-reduce.6.cloned.1.call-start = ((), (), s32[]{:S(2)}) async-start(), calls=%async_computation.4 | async-start | bytes 1048576
  30.0 96.8 %all-reduce.4.cloned.1.call-start = ((), (), s32[]{:S(2)}) async-start(), calls=%async_computation.3 | async-start | bytes 131072 | tf_op jit(solution)/shard_map/psum | solution.py:66
  30.0 0.7 copy-start.2
  32.0 3.7 %collective-permute-start = (bf16[64,2,128]{2,0,1:T(8,128)(2,1)S(1)}, bf16[64,2,128]{2,0,1:T(8,128)(2,1)S(1)}, u32[]{:S(2)}, u32[]{:S(2)}) collective-permute-start(bf16[64,2,128]{2,0,1:T(8,128)(2,1)S(1)} %slice.8), channel_id=1, source_target_pairs={{0,2},{2,4},{4,6},{1,3},{3,5},{5,7},{8,10},{10,12},{12,14},{9,11},... | collective-permute-start | bytes 98312 | tf_op jit(solution)/shard_map/ppermute | solution.py:14
Sparse Core Ops, SparseCore 0:
  33.1 57.0 all-reduce.5
  93.1 33.6 all-reduce.3
where the time goes:
time: 136 us; the launch traced here: 135 us
  waiting for transfers between devices  86 us (63%)
  starting transfers between devices  15.5 us (11%)
  between operations  14.9 us (11%)
  local copies, waits for them, and re-layouts  11.1 us (8%)
  loops' own time  2.97 us (2%)
  matrix products  2.88 us (2%)
  other arithmetic  1.87 us (1%)
    unnamed x3, waiting for transfers between devices  52.3 us
    psum x1, waiting for transfers between devices, average(): total = lax.psum(share, 'dp')  24.8 us
    all_to_all x1, starting transfers between devices, attend(): lax.all_to_all(k_heads, 'aa', split_axis=1, concat_axis=0, tiled=True)  4.37 us
    ppermute x2, starting transfers between devices, shifted(): return lax.ppermute(value, axis, pairs)  4.15 us
    unnamed x11, local copies, waits for them, and re-layouts  4.12 us
    all_to_all x1, waiting for transfers between devices, attend(): lax.all_to_all(k_heads, 'aa', split_axis=1, concat_axis=0, tiled=True)  3.66 us
    all_to_all x1, starting transfers between devices, attend(): lax.all_to_all(q_heads, 'aa', split_axis=1, concat_axis=0, tiled=True)  3.49 us
    all_to_all x1, starting transfers between devices, attend(): lax.all_to_all(v_heads, 'aa', split_axis=1, concat_axis=0, tiled=True)  3.38 us
  transfers between devices with their start and end apart: 7, of which 6 were waited for; matrix products, arithmetic and copies ran while one was open for 8% of the time, Pallas kernels for 0%

commit v1 on v0

--- a/solution.py
+++ b/solution.py
@@ -1,11 +1,17 @@
+import functools
+
 import jax
 import jax.numpy as jnp
 from jax import lax
+from jax.experimental import pallas as pl
+from jax.experimental.pallas import tpu as pltpu
 from jax.sharding import PartitionSpec as P
 
 HQ = 16
 KVH = 4
 DH = 128
+LANES = 128
+MESH = pl.DeviceIdType.MESH
 
 
 def shifted(value, axis, by):
@@ -73,6 +79,281 @@
     return (attended, grad_mean)
 
 
+def fused_kernel(
+    sizes, q_hbm, k_hbm, v_hbm, g_hbm, out_ref, mean_ref,
+    q_ref, k_ref, v_ref, g_ref, o_send, o_own, m_own, g1_send, g1_recv, g2_send, g2_recv, g3,
+    load_sem, halo_send, halo_recv, o_send_sem, o_recv_sem, own_sem,
+    g1_sem, g2_send_sem, g2_recv_sem, g3_send_sem, g3_recv_sem,
+):
+    n_dp, n_blk, n_aa = sizes
+    tok = q_hbm.shape[0]
+    reach = tok // 2
+    group = HQ // KVH
+    kv_here = KVH // n_aa
+    wide = group * DH
+    n_y = n_blk // 2
+    plane = n_y * n_aa
+    share = g2_send.shape[1]
+    dp, blk, aa = lax.axis_index("dp"), lax.axis_index("blk"), lax.axis_index("aa")
+    core, y = blk % 2, blk // 2
+    other = 1 - aa
+    place = blk * n_aa + aa
+    last = n_blk * n_aa - 1
+    spot = y * n_aa + aa
+
+    loads = [
+        pltpu.make_async_copy(k_hbm, k_ref.at[pl.ds(reach, tok)], load_sem.at[0]),
+        pltpu.make_async_copy(v_hbm, v_ref.at[pl.ds(reach, tok)], load_sem.at[1]),
+        pltpu.make_async_copy(g_hbm, g_ref, load_sem.at[2]),
+        pltpu.make_async_copy(q_hbm, q_ref, load_sem.at[3]),
+    ]
+    for load in loads:
+        load.start()
+
+    partner = (dp, blk + 1 - 2 * core, aa)
+
+    def plane_peer(d):
+        to = (spot + d) % plane
+        return to, (dp, (to // n_aa) * 2 + core, to % n_aa)
+
+    def dp_peer(d):
+        return ((dp + d) % n_dp, blk, aa)
+
+    def at_place(p):
+        return (dp, p // n_aa, p % n_aa)
+
+    barrier = pltpu.get_barrier_semaphore()
+    greeted = [partner] + [plane_peer(d)[1] for d in range(1, plane)]
+    greeted += [dp_peer(d) for d in range(1, n_dp)]
+    for peer in greeted:
+        pl.semaphore_signal(barrier, inc=1, device_id=peer, device_id_type=MESH)
+    ahead = (aa == n_aa - 1) & (place < last)
+    behind = (aa == 0) & (place > 0)
+
+    @pl.when(ahead)
+    def _():
+        pl.semaphore_signal(barrier, inc=1, device_id=at_place(place + 1), device_id_type=MESH)
+
+    @pl.when(behind)
+    def _():
+        pl.semaphore_signal(barrier, inc=1, device_id=at_place(place - 1), device_id_type=MESH)
+
+    @pl.when(place == 0)
+    def _():
+        k_ref[0:reach] = jnp.zeros((reach, KVH * DH), k_ref.dtype)
+        v_ref[0:reach] = jnp.zeros((reach, KVH * DH), v_ref.dtype)
+
+    def rows_of(y_at, core_at):
+        return pl.ds(pl.multiple_of((y_at * 2 + core_at) * n_aa * share, share), n_aa * share)
+
+    loads[2].wait()
+    for y_at in range(n_y):
+        g1_send[y_at] = g_ref[rows_of(y_at, 1 - core)].astype(jnp.bfloat16)
+    loads[0].wait()
+    loads[1].wait()
+
+    @pl.when(ahead | behind)
+    def _():
+        pl.semaphore_wait(barrier, len(greeted) + 1)
+
+    @pl.when(jnp.logical_not(ahead | behind))
+    def _():
+        pl.semaphore_wait(barrier, len(greeted))
+
+    def remote(src, dst, send_sem, recv_sem, to):
+        return pltpu.make_async_remote_copy(
+            src_ref=src, dst_ref=dst, send_sem=send_sem, recv_sem=recv_sem,
+            device_id=to, device_id_type=MESH,
+        )
+
+    first = remote(g1_send, g1_recv, g1_sem.at[0], g1_sem.at[1], partner)
+    first.start()
+
+    def halo(ref, i):
+        return remote(
+            ref.at[pl.ds(tok, reach)], ref.at[pl.ds(0, reach)],
+            halo_send.at[i], halo_recv.at[i], at_place(jnp.minimum(place + 1, last)),
+        )
+
+    @pl.when(place < last)
+    def _():
+        halo(k_ref, 0).start()
+        halo(v_ref, 1).start()
+
+    def unit(block, kv, target):
+        kv_at = target * kv_here + kv
+        rows = pl.ds(block * reach, reach)
+        span = pl.ds(block * reach, 2 * reach)
+        q_cols = pl.multiple_of(kv_at * wide, wide)
+        kv_cols = pl.ds(pl.multiple_of(kv_at * DH, DH), DH)
+        q_all = q_ref[rows, pl.ds(q_cols, wide)]
+        q = jnp.concatenate([q_all[:, h * DH : (h + 1) * DH] for h in range(group)], 0)
+        scores = lax.dot_general(
+            q, k_ref[span, kv_cols], (((1,), (1,)), ((), ())), preferred_element_type=jnp.float32
+        ) * (DH ** -0.5)
+        i = lax.broadcasted_iota(jnp.int32, scores.shape, 0) % reach
+        j = lax.broadcasted_iota(jnp.int32, scores.shape, 1)
+        scores = jnp.where((j > i) & (j <= i + reach), scores, -1e30)
+        expo = jnp.exp(scores - jnp.max(scores, axis=-1, keepdims=True))
+        weights = (expo / jnp.sum(expo, axis=-1, keepdims=True)).astype(jnp.bfloat16)
+        out = jnp.dot(weights, v_ref[span, kv_cols], preferred_element_type=jnp.float32)
+        out = out.astype(jnp.bfloat16)
+        return jnp.concatenate([out[h * reach : (h + 1) * reach] for h in range(group)], 1)
+
+    def send_out(block, kv):
+        cols = pl.ds(kv * wide, wide)
+        start = pl.multiple_of(aa * tok + block * reach, reach)
+        at = block * kv_here + kv
+        return remote(
+            o_send.at[pl.ds(block * reach, reach), cols], out_ref.at[pl.ds(start, reach), cols],
+            o_send_sem.at[at], o_recv_sem.at[at], (dp, blk, other),
+        )
+
+    def for_other(block):
+        for kv in range(kv_here):
+            o_send[pl.ds(block * reach, reach), pl.ds(kv * wide, wide)] = unit(block, kv, other)
+
+    def for_self(block):
+        for kv in range(kv_here):
+            o_own[pl.ds(block * reach, reach), pl.ds(kv * wide, wide)] = unit(block, kv, aa)
+
+    loads[3].wait()
+    for_other(1)
+
+    first.wait_recv()
+    for y_at in range(n_y):
+        summed = g_ref[rows_of(y_at, core)] + g1_recv[y_at].astype(jnp.float32)
+        for a_at in range(n_aa):
+            g2_send[y_at * n_aa + a_at] = summed[a_at * share : (a_at + 1) * share].astype(jnp.bfloat16)
+
+    def second(d):
+        to, peer = plane_peer(d)
+        return remote(
+            g2_send.at[to], g2_recv.at[d - 1], g2_send_sem.at[d - 1], g2_recv_sem.at[d - 1], peer
+        )
+
+    for d in range(1, plane):
+        second(d).start()
+    for kv in range(kv_here):
+        send_out(1, kv).start()
+    for_self(1)
+
+    @pl.when(place > 0)
+    def _():
+        halo(k_ref, 0).wait_recv()
+        halo(v_ref, 1).wait_recv()
+
+    for_other(0)
+    for kv in range(kv_here):
+        send_out(0, kv).start()
+
+    own_rows = pl.ds(pl.multiple_of(place * share, share), share)
+    own = g_ref[own_rows] + g1_recv[y, pl.ds(pl.multiple_of(aa * share, share), share)].astype(jnp.float32)
+    for d in range(1, plane):
+        second(d).wait_recv()
+        own = own + g2_recv[d - 1].astype(jnp.float32)
+    g3[dp] = own.astype(jnp.bfloat16)
+
+    def third(d):
+        return remote(
+            g3.at[dp], g3.at[dp], g3_send_sem.at[d - 1], g3_recv_sem.at[d - 1], dp_peer(d)
+        )
+
+    def third_in(d):
+        origin = (dp + n_dp - d) % n_dp
+        return remote(
+            g3.at[origin], g3.at[origin], g3_send_sem.at[d - 1], g3_recv_sem.at[d - 1], dp_peer(d)
+        )
+
+    for d in range(1, n_dp):
+        third(d).start()
+
+    for_self(0)
+    own_out = pltpu.make_async_copy(
+        o_own, out_ref.at[pl.ds(pl.multiple_of(aa * tok, tok), tok)], own_sem.at[0]
+    )
+    own_out.start()
+
+    for d in range(1, n_dp):
+        third_in(d).wait_recv()
+    total = g3[0].astype(jnp.float32)
+    for z in range(1, n_dp):
+        total = total + g3[z].astype(jnp.float32)
+    m_own[...] = total / (n_dp * n_blk * n_aa)
+    mean_out = pltpu.make_async_copy(m_own, mean_ref, own_sem.at[1])
+    mean_out.start()
+
+    first.wait_send()
+
+    @pl.when(place < last)
+    def _():
+        halo(k_ref, 0).wait_send()
+        halo(v_ref, 1).wait_send()
+
+    for d in range(1, plane):
+        second(d).wait_send()
+    for d in range(1, n_dp):
+        third(d).wait_send()
+    for block in (1, 0):
+        for kv in range(kv_here):
+            send_out(block, kv).wait()
+    own_out.wait()
+    mean_out.wait()
+
+
+def fused(sizes, queries, keys, values, grad_parts):
+    n_dp, n_blk, n_aa = sizes
+    tok, q_width = queries.shape[1:]
+    reach = tok // 2
+    rows = grad_parts.size // LANES
+    share = rows // (n_blk * n_aa)
+    plane = n_blk // 2 * n_aa
+    kv_here = KVH // n_aa
+    bf16, f32 = jnp.bfloat16, jnp.float32
+    dma = lambda *shape: pltpu.SemaphoreType.DMA(shape)
+    hbm = pl.BlockSpec(memory_space=pl.ANY)
+    attended, mean = pl.pallas_call(
+        functools.partial(fused_kernel, sizes),
+        out_shape=(
+            jax.ShapeDtypeStruct((tok * n_aa, q_width // n_aa), bf16),
+            jax.ShapeDtypeStruct((share, LANES), f32),
+        ),
+        in_specs=[hbm] * 4,
+        out_specs=(hbm, hbm),
+        scratch_shapes=[
+            pltpu.VMEM((tok, q_width), bf16),
+            pltpu.VMEM((reach + tok, KVH * DH), bf16),
+            pltpu.VMEM((reach + tok, KVH * DH), bf16),
+            pltpu.VMEM((rows, LANES), f32),
+            pltpu.VMEM((tok, q_width // n_aa), bf16),
+            pltpu.VMEM((tok, q_width // n_aa), bf16),
+            pltpu.VMEM((share, LANES), f32),
+            pltpu.VMEM((n_blk // 2, n_aa * share, LANES), bf16),
+            pltpu.VMEM((n_blk // 2, n_aa * share, LANES), bf16),
+            pltpu.VMEM((plane, share, LANES), bf16),
+            pltpu.VMEM((plane - 1, share, LANES), bf16),
+            pltpu.VMEM((n_dp, share, LANES), bf16),
+            dma(4), dma(2), dma(2), dma(2 * kv_here), dma(2 * kv_here), dma(2),
+            dma(2), dma(plane - 1), dma(plane - 1), dma(n_dp - 1), dma(n_dp - 1),
+        ],
+        compiler_params=pltpu.CompilerParams(collective_id=0, has_side_effects=True),
+        name="fused",
+    )(queries[0], keys[0], values[0], grad_parts.reshape(rows, LANES))
+    return attended[None], mean.reshape(-1)
+
+
+def fits(sizes, args):
+    n_dp, n_blk, n_aa = sizes
+    queries, _, _, grad_parts = args
+    rows, rest = divmod(grad_parts.shape[-1], LANES)
+    shares = n_blk * n_aa
+    tokens = queries.shape[1] // shares
+    return (
+        n_aa == 2 and n_blk % 2 == 0 and n_dp > 1 and KVH % n_aa == 0
+        and tokens % 32 == 0 and rest == 0 and rows % (shares * 16) == 0
+    )
+
+
 def solution(mesh):
     placed = (
         P("dp", ("blk", "aa"), None),
@@ -80,10 +361,16 @@
         P("dp", ("blk", "aa"), None),
         P("dp", ("blk", "aa"), None),
     )
-    return jax.shard_map(
-        shards,
-        mesh=mesh,
-        in_specs=placed,
-        out_specs=(P("dp", "blk", "aa"), P(("blk", "aa"))),
-        check_vma=False,
-    )
+    sizes = tuple(mesh.shape[axis] for axis in ("dp", "blk", "aa"))
+
+    def step(*args):
+        body = functools.partial(fused, sizes) if fits(sizes, args) else shards
+        return jax.shard_map(
+            body,
+            mesh=mesh,
+            in_specs=placed,
+            out_specs=(P("dp", "blk", "aa"), P(("blk", "aa"))),
+            check_vma=False,
+        )(*args)
+
+    return step

time: 136 us -> 20.7 us (0.15)
  waiting for transfers between devices: 86 us -> 0 us
  Pallas kernels: 0 us -> 17.3 us
  starting transfers between devices: 15.5 us -> 0 us
  between operations: 14.9 us -> 0.65 us
  local copies, waits for them, and re-layouts: 11.1 us -> 2.54 us
  loops' own time: 2.97 us -> 0 us
  matrix products: 2.88 us -> 0 us
  other arithmetic: 1.87 us -> 0 us
    unnamed x3 -> x0, waiting for transfers between devices: 52.3 us -> none
    psum x1 -> x0, waiting for transfers between devices: 24.8 us -> none  [average(): total = lax.psum(share, 'dp')]
    pallas_call x0 -> x1, Pallas kernels: none -> 17.3 us  [fused(): pl.pallas_call(functools.partial(fused_kernel, sizes), out_shape=(jax.Sha...]
    all_to_all x3 -> x0, starting transfers between devices: 11.2 us -> none  [the longest x1 4.37 us: attend(): lax.all_to_all(k_heads, 'aa', split_axis=1, concat_axis=0, tiled=True)]
    all_to_all x3 -> x0, waiting for transfers between devices: 8.16 us -> none  [the longest x1 3.66 us: attend(): lax.all_to_all(k_heads, 'aa', split_axis=1, concat_axis=0, tiled=True)]
    ppermute x2 -> x0, starting transfers between devices: 4.15 us -> none  [shifted(): return lax.ppermute(value, axis, pairs)]
    another operation x4 -> x0, local copies, waits for them, and re-layouts: 3.58 us -> none  [the longest x1 1.02 us: shards(): attended = attend(queries[0], keys[0], values[0])[None]]
    another operation x1 -> x0, loops' own time: 2.97 us -> none  [attend(): blocks = lax.map(one_block, jnp.arange(span // step_rows, dtype=jnp.int32))]
  transfers between devices with their start and end apart: 7 -> 0, of which waited for: 6 -> 0; matrix products, arithmetic and copies ran while one was open for 8% -> 0% of each run, Pallas kernels for 0% -> 0%
where the time goes in v1:
time: 20.7 us; the launch traced here: 20.5 us
  Pallas kernels  17.3 us (84%)
  local copies, waits for them, and re-layouts  2.54 us (12%)
  between operations  0.65 us (3%)
    pallas_call x1, Pallas kernels, fused(): pl.pallas_call(functools.partial(fused_kernel, sizes), out_shape=(jax.Sha...  17.3 us
    unnamed x4, local copies, waits for them, and re-layouts  2.54 us

profile of v1, /device:TPU:0, one launch (start us, length us, event | category | flops | bytes accessed | tf_op | source)
XLA Modules:
  0.0 20.5 jit_solution(15081972720668717564)
XLA Ops:
  0.6 17.3 %fused.1 = (bf16[256,1024]{1,0:T(8,128)(2,1)}, f32[128,128]{1,0:T(8,128)}) custom-call(bf16[128,2048]{1,0:T(8,128)(2,1)} %bitcast.6, bf16[128,512]{1,0:T(8,128)(2,1)} %bitcast.9, bf16[128,512]{1,0:T(8,128)(2,1)} %bitcast.10, f32[1024,128]{1,0:T(8,128)} %bitcast.7), custom_call_target="tpu_custom_call" | custom-call | tf_op jit(solution)/shard_map/fused/pallas_call | solution.py:315
  17.9 0.0 copy-start
  18.0 1.9 %copy.8 = bf16[1,256,1024]{2,1,0:T(8,128)(2,1)} copy(bf16[1,256,1024]{2,1,0:T(8,128)(2,1)} %bitcast.8) | data formatting | bytes 1048576
  19.9 0.0 copy-done
  19.9 0.6 %copy.9 = f32[16384]{0:T(1024)} copy(f32[16384]{0:T(1024)S(1)} %bitcast.11) | data formatting | bytes 131072
Async XLA Ops:
  17.9 1.9 %copy-start = (f32[128,128]{1,0:T(8,128)S(1)}, f32[128,128]{1,0:T(8,128)}, u32[]{:S(2)}) copy-start(f32[128,128]{1,0:T(8,128)} %get-tuple-element.5) | copy-start | bytes 196612

commit v2 on v1

--- a/solution.py
+++ b/solution.py
@@ -81,8 +81,8 @@
 
 def fused_kernel(
     sizes, q_hbm, k_hbm, v_hbm, g_hbm, out_ref, mean_ref,
-    q_ref, k_ref, v_ref, g_ref, o_send, o_own, m_own, g1_send, g1_recv, g2_send, g2_recv, g3,
-    load_sem, halo_send, halo_recv, o_send_sem, o_recv_sem, own_sem,
+    q_ref, k_ref, v_ref, g_ref, o_send, g1_send, g1_recv, g2_send, g2_recv, g3,
+    load_sem, halo_send, halo_recv, o_send_sem, o_recv_sem,
     g1_sem, g2_send_sem, g2_recv_sem, g3_send_sem, g3_recv_sem,
 ):
     n_dp, n_blk, n_aa = sizes
@@ -215,7 +215,8 @@
 
     def for_self(block):
         for kv in range(kv_here):
-            o_own[pl.ds(block * reach, reach), pl.ds(kv * wide, wide)] = unit(block, kv, aa)
+            start = pl.multiple_of(aa * tok + block * reach, reach)
+            out_ref[pl.ds(start, reach), pl.ds(kv * wide, wide)] = unit(block, kv, aa)
 
     loads[3].wait()
     for_other(1)
@@ -269,19 +270,12 @@
         third(d).start()
 
     for_self(0)
-    own_out = pltpu.make_async_copy(
-        o_own, out_ref.at[pl.ds(pl.multiple_of(aa * tok, tok), tok)], own_sem.at[0]
-    )
-    own_out.start()
-
     for d in range(1, n_dp):
         third_in(d).wait_recv()
     total = g3[0].astype(jnp.float32)
     for z in range(1, n_dp):
         total = total + g3[z].astype(jnp.float32)
-    m_own[...] = total / (n_dp * n_blk * n_aa)
-    mean_out = pltpu.make_async_copy(m_own, mean_ref, own_sem.at[1])
-    mean_out.start()
+    mean_ref[...] = total / (n_dp * n_blk * n_aa)
 
     first.wait_send()
 
@@ -297,8 +291,15 @@
     for block in (1, 0):
         for kv in range(kv_here):
             send_out(block, kv).wait()
-    own_out.wait()
-    mean_out.wait()
+
+
+def finish_kernel(out_in, mean_in, out_ref, mean_ref, sem):
+    out_copy = pltpu.make_async_copy(out_in, out_ref, sem.at[0])
+    mean_copy = pltpu.make_async_copy(mean_in, mean_ref, sem.at[1])
+    out_copy.start()
+    mean_copy.start()
+    out_copy.wait()
+    mean_copy.wait()
 
 
 def fused(sizes, queries, keys, values, grad_parts):
@@ -311,34 +312,42 @@
     kv_here = KVH // n_aa
     bf16, f32 = jnp.bfloat16, jnp.float32
     dma = lambda *shape: pltpu.SemaphoreType.DMA(shape)
+    vmem = pl.BlockSpec(memory_space=pltpu.VMEM)
     hbm = pl.BlockSpec(memory_space=pl.ANY)
     attended, mean = pl.pallas_call(
         functools.partial(fused_kernel, sizes),
         out_shape=(
-            jax.ShapeDtypeStruct((tok * n_aa, q_width // n_aa), bf16),
-            jax.ShapeDtypeStruct((share, LANES), f32),
+            pltpu.VMEM((tok * n_aa, q_width // n_aa), bf16),
+            pltpu.VMEM((share, LANES), f32),
         ),
         in_specs=[hbm] * 4,
-        out_specs=(hbm, hbm),
+        out_specs=(vmem, vmem),
         scratch_shapes=[
             pltpu.VMEM((tok, q_width), bf16),
             pltpu.VMEM((reach + tok, KVH * DH), bf16),
             pltpu.VMEM((reach + tok, KVH * DH), bf16),
             pltpu.VMEM((rows, LANES), f32),
             pltpu.VMEM((tok, q_width // n_aa), bf16),
-            pltpu.VMEM((tok, q_width // n_aa), bf16),
-            pltpu.VMEM((share, LANES), f32),
             pltpu.VMEM((n_blk // 2, n_aa * share, LANES), bf16),
             pltpu.VMEM((n_blk // 2, n_aa * share, LANES), bf16),
             pltpu.VMEM((plane, share, LANES), bf16),
             pltpu.VMEM((plane - 1, share, LANES), bf16),
             pltpu.VMEM((n_dp, share, LANES), bf16),
-            dma(4), dma(2), dma(2), dma(2 * kv_here), dma(2 * kv_here), dma(2),
+            dma(4), dma(2), dma(2), dma(2 * kv_here), dma(2 * kv_here),
             dma(2), dma(plane - 1), dma(plane - 1), dma(n_dp - 1), dma(n_dp - 1),
         ],
         compiler_params=pltpu.CompilerParams(collective_id=0, has_side_effects=True),
         name="fused",
     )(queries[0], keys[0], values[0], grad_parts.reshape(rows, LANES))
+    attended, mean = pl.pallas_call(
+        finish_kernel,
+        out_shape=tuple(jax.ShapeDtypeStruct(a.shape, a.dtype) for a in (attended, mean)),
+        in_specs=[hbm] * 2,
+        out_specs=(hbm, hbm),
+        scratch_shapes=[dma(2)],
+        compiler_params=pltpu.CompilerParams(vmem_limit_bytes=1024 * 1024),
+        name="finish",
+    )(attended, mean)
     return attended[None], mean.reshape(-1)
 
 

time: 20.7 us -> 18.8 us (0.908)
  local copies, waits for them, and re-layouts: 2.54 us -> 0 us
  Pallas kernels: 17.3 us -> 18 us
    unnamed x4 -> x0, local copies, waits for them, and re-layouts: 2.54 us -> none
    pallas_call x1 -> x2, Pallas kernels: 17.3 us -> 18 us  [the longest x1 17.2 us: fused(): pl.pallas_call(functools.partial(fused_kernel, sizes), out_shape=(pltpu.V...]
where the time goes in v2:
time: 18.8 us; the launch traced here: 18.6 us
  Pallas kernels  18 us (96%)
  between operations  0.64 us (3%)
    pallas_call x1, Pallas kernels, fused(): pl.pallas_call(functools.partial(fused_kernel, sizes), out_shape=(pltpu.V...  17.2 us
    pallas_call x1, Pallas kernels, fused(): pl.pallas_call(finish_kernel, out_shape=tuple((jax.ShapeDtypeStruct(a.sha...  0.82 us

profile of v2, /device:TPU:0, one launch (start us, length us, event | category | flops | bytes accessed | tf_op | source)
XLA Modules:
  0.0 18.6 jit_solution(15664937788346342088)
XLA Ops:
  0.6 17.2 %fused.1 = (bf16[256,1024]{1,0:T(8,128)(2,1)S(1)}, f32[128,128]{1,0:T(8,128)S(1)}) custom-call(bf16[128,2048]{1,0:T(8,128)(2,1)} %bitcast.6, bf16[128,512]{1,0:T(8,128)(2,1)} %bitcast.8, bf16[128,512]{1,0:T(8,128)(2,1)} %bitcast.9, f32[1024,128]{1,0:T(8,128)} %bitcast.7), custom_call_target="tpu_custom_call" | custom-call | tf_op jit(solution)/shard_map/fused/pallas_call | solution.py:317
  17.8 0.8 %finish.1 = (bf16[256,1024]{1,0:T(8,128)(2,1)}, f32[128,128]{1,0:T(8,128)}) custom-call(bf16[256,1024]{1,0:T(8,128)(2,1)S(1)} %get-tuple-element.6.out_in, f32[128,128]{1,0:T(8,128)S(1)} %get-tuple-element.7.mean_in), custom_call_target="tpu_custom_call" | custom-call | tf_op jit(solution)/shard_map/finish/pallas_call | solution.py:342

commit v3 on v2

--- a/solution.py
+++ b/solution.py
@@ -83,7 +83,7 @@
     sizes, q_hbm, k_hbm, v_hbm, g_hbm, out_ref, mean_ref,
     q_ref, k_ref, v_ref, g_ref, o_send, g1_send, g1_recv, g2_send, g2_recv, g3,
     load_sem, halo_send, halo_recv, o_send_sem, o_recv_sem,
-    g1_sem, g2_send_sem, g2_recv_sem, g3_send_sem, g3_recv_sem,
+    g1_sem, g2_send_sem, g2_recv_sem, g3_send_sem, g3_recv_sem, far_sem,
 ):
     n_dp, n_blk, n_aa = sizes
     tok = q_hbm.shape[0]
@@ -124,11 +124,18 @@
 
     barrier = pltpu.get_barrier_semaphore()
     greeted = [partner] + [plane_peer(d)[1] for d in range(1, plane)]
-    greeted += [dp_peer(d) for d in range(1, n_dp)]
     for peer in greeted:
         pl.semaphore_signal(barrier, inc=1, device_id=peer, device_id_type=MESH)
     ahead = (aa == n_aa - 1) & (place < last)
     behind = (aa == 0) & (place > 0)
+
+    @pl.when(dp > 0)
+    def _():
+        pl.semaphore_signal(barrier, inc=1, device_id=(dp - 1, blk, aa), device_id_type=MESH)
+
+    @pl.when(dp < n_dp - 1)
+    def _():
+        pl.semaphore_signal(barrier, inc=1, device_id=(dp + 1, blk, aa), device_id_type=MESH)
 
     @pl.when(ahead)
     def _():
@@ -152,13 +159,30 @@
     loads[0].wait()
     loads[1].wait()
 
-    @pl.when(ahead | behind)
-    def _():
-        pl.semaphore_wait(barrier, len(greeted) + 1)
-
-    @pl.when(jnp.logical_not(ahead | behind))
-    def _():
-        pl.semaphore_wait(barrier, len(greeted))
+    extra = [ahead | behind, dp > 0, dp < n_dp - 1]
+    pl.semaphore_wait(barrier, len(greeted) + sum(e.astype(jnp.int32) for e in extra))
+
+    def tell(k):
+        @pl.when((dp > 0) & (dp + 1 + k < n_dp))
+        def _():
+            pl.semaphore_signal(
+                far_sem.at[0, k], inc=1, device_id=(dp - 1, blk, aa), device_id_type=MESH
+            )
+
+        @pl.when((dp < n_dp - 1) & (dp - 1 - k >= 0))
+        def _():
+            pl.semaphore_signal(
+                far_sem.at[1, k], inc=1, device_id=(dp + 1, blk, aa), device_id_type=MESH
+            )
+
+    def hear(k):
+        @pl.when(dp + 2 + k < n_dp)
+        def _():
+            pl.semaphore_wait(far_sem.at[0, k], 1)
+
+        @pl.when(dp - 2 - k >= 0)
+        def _():
+            pl.semaphore_wait(far_sem.at[1, k], 1)
 
     def remote(src, dst, send_sem, recv_sem, to):
         return pltpu.make_async_remote_copy(
@@ -168,6 +192,8 @@
 
     first = remote(g1_send, g1_recv, g1_sem.at[0], g1_sem.at[1], partner)
     first.start()
+    if n_dp > 2:
+        tell(0)
 
     def halo(ref, i):
         return remote(
@@ -238,6 +264,9 @@
     for kv in range(kv_here):
         send_out(1, kv).start()
     for_self(1)
+    for k in range(1, n_dp - 2):
+        hear(k - 1)
+        tell(k)
 
     @pl.when(place > 0)
     def _():
@@ -266,6 +295,8 @@
             g3.at[origin], g3.at[origin], g3_send_sem.at[d - 1], g3_recv_sem.at[d - 1], dp_peer(d)
         )
 
+    if n_dp > 2:
+        hear(n_dp - 3)
     for d in range(1, n_dp):
         third(d).start()
 
@@ -335,6 +366,7 @@
             pltpu.VMEM((n_dp, share, LANES), bf16),
             dma(4), dma(2), dma(2), dma(2 * kv_here), dma(2 * kv_here),
             dma(2), dma(plane - 1), dma(plane - 1), dma(n_dp - 1), dma(n_dp - 1),
+            pltpu.SemaphoreType.REGULAR((2, max(n_dp - 2, 1))),
         ],
         compiler_params=pltpu.CompilerParams(collective_id=0, has_side_effects=True),
         name="fused",

time: 18.8 us -> 17.8 us (0.947)
  Pallas kernels: 18 us -> 17 us
    pallas_call x1, Pallas kernels: 17.2 us -> 16.2 us  [fused(): pl.pallas_call(functools.partial(fused_kernel, sizes), out_shape=(pltpu.V...]
where the time goes in v3:
time: 17.8 us; the launch traced here: 17.6 us
  Pallas kernels  17 us (96%)
  between operations  0.64 us (4%)
    pallas_call x1, Pallas kernels, fused(): pl.pallas_call(functools.partial(fused_kernel, sizes), out_shape=(pltpu.V...  16.2 us
    pallas_call x1, Pallas kernels, fused(): pl.pallas_call(finish_kernel, out_shape=tuple((jax.ShapeDtypeStruct(a.sha...  0.82 us

profile of v3, /device:TPU:0, one launch (start us, length us, event | category | flops | bytes accessed | tf_op | source)
XLA Modules:
  0.0 17.6 jit_solution(15344309609073948499)
XLA Ops:
  0.6 16.2 %fused.1 = (bf16[256,1024]{1,0:T(8,128)(2,1)S(1)}, f32[128,128]{1,0:T(8,128)S(1)}) custom-call(bf16[128,2048]{1,0:T(8,128)(2,1)} %bitcast.6, bf16[128,512]{1,0:T(8,128)(2,1)} %bitcast.8, bf16[128,512]{1,0:T(8,128)(2,1)} %bitcast.9, f32[1024,128]{1,0:T(8,128)} %bitcast.7), custom_call_target="tpu_custom_call" | custom-call | tf_op jit(solution)/shard_map/fused/pallas_call | solution.py:348
  16.8 0.8 %finish.1 = (bf16[256,1024]{1,0:T(8,128)(2,1)}, f32[128,128]{1,0:T(8,128)}) custom-call(bf16[256,1024]{1,0:T(8,128)(2,1)S(1)} %get-tuple-element.6.out_in, f32[128,128]{1,0:T(8,128)S(1)} %get-tuple-element.7.mean_in), custom_call_target="tpu_custom_call" | custom-call | tf_op jit(solution)/shard_map/finish/pallas_call | solution.py:374
